TPU v7x, 32 devices: a whole 2x2x4 slice. The times are simulated.
32 devices in a mesh: pair: 2 (over core), shard: 16 (over z, y, x).
Axes of the slice: x: 2, y: 2, z: 4, core: 2. Of those that a mesh axis runs over, the one named last changes fastest.
Arguments:
- master: float32 [3072, 4096], P('shard', 'pair'), may hold values from -1.5 to 1.5
- gradient: float32 [3072, 4096], P('shard', 'pair'), may hold values from -40 to 40
- first_moment: float32 [3072, 4096], P('shard', 'pair'), may hold values from -4 to 4
- second_moment: float32 [3072, 4096], P('shard', 'pair'), may hold values from 0.02 to 4
- max_norm: float32 [1], replicated, may hold values from 768 to 1536
- step_count: int32 [1], replicated, may hold values from 1 to 1000
Outputs:
- new_master: float32 [3072, 4096], P('shard', 'pair')
- new_first: float32 [3072, 4096], P('shard', 'pair')
- new_second: float32 [3072, 4096], P('shard', 'pair')
- compute_codes: bfloat16 [3072, 4096], P('pair')
- block_scales: bfloat16 [3072, 128], P('pair')
All inputs are finite; a program needn't handle non-finite values.
Results may differ from a plain program's by a relative error of at most 0.001.
The roundings to bfloat16 on the way count: a program that leaves them out, or rounds other values in their place, can miss the bound.
Values may be sent and summed in bfloat16 or wider, within the bound.
A program may use at most 192 MiB of HBM per device.

v0:
```python
import functools

import jax
import jax.numpy as jnp
from jax import lax
from jax.experimental import pallas as pl
from jax.experimental.pallas import tpu as pltpu
from jax.sharding import PartitionSpec as P

BLOCK = 32
LANES = 128

beta_first = 0.9
beta_second = 0.99
learn_rate = 0.01
decay_rate = 0.1
adam_eps = 1e-06
scale_floor = 0.25

MESH = pl.DeviceIdType.MESH
Z, Y, X = 0, 1, 2
PIECES = (
    ((Z, X, Y), 3),
    ((Z, Y, X), 3),
    ((X, Y, Z), 2),
    ((Z, X, Y), 3),
    ((Z, Y, X), 3),
    ((Y, X, Z), 2),
)
SCALE_ORDER = (Z, X, Y)
WINDOW = 8


def grid_of(mesh):
    count = mesh.shape["shard"]
    at = [d.coords for d in mesh.devices.reshape(mesh.shape["pair"], count)[0]]
    sizes = tuple(len({c[d] for c in at}) for d in (2, 1, 0))
    return sizes


def power(base, exponent):
    result = jnp.float32(1.0)
    for bit in range(31):
        factor = jnp.float32(base ** (2**bit))
        result = jnp.where((exponent >> bit) & 1 == 1, result * factor, result)
    return result


def kernel(
    grid, limit_ref, step_ref, master_hbm, gradient_hbm, first_hbm, second_hbm,
    new_master, new_first, new_second, codes, scales,
    master, gradient, first, second, mine, my_scales, wide_scales, their_scales,
    plane_sums, line_sums,
    load_sem, plane_send, plane_recv, line_send, line_recv,
    own_send, own_scale_send, peer_send, peer_scale_send, peer_scale_recv,
    pass_send, pass_scale_send, code_recv, scale_recv, local_sem,
):
    sizes = grid
    depth, high, wide = sizes
    plane = high * wide
    half_depth = depth // 2
    sources = half_depth * plane
    height, width = mine.shape
    tiles = width // LANES
    core = lax.axis_index("pair")
    chip = lax.axis_index("shard")
    here = (chip // plane, (chip // wide) % high, chip % wide)
    keeper = here[Z] // half_depth
    peer = 1 - core

    def chip_at(at):
        return (at[Z] * high + at[Y]) * wide + at[X]

    loads = [
        pltpu.make_async_copy(source, held, load_sem.at[i])
        for i, (source, held) in enumerate(
            ((gradient_hbm, gradient), (master_hbm, master), (first_hbm, first), (second_hbm, second))
        )
    ]
    for load in loads:
        load.start()

    barrier = pltpu.get_barrier_semaphore()
    group = 2 * plane
    my_place = core * plane + here[Y] * wide + here[X]

    def greet(device):
        pl.semaphore_signal(barrier, inc=1, device_id=device, device_id_type=MESH)

    for place in range(group):
        @pl.when(place != my_place)
        def _():
            greet((place // plane, here[Z] * plane + place % plane))

    for other in range(depth):
        for side in range(2):
            @pl.when(other != here[Z])
            def _():
                greet((side, chip_at((other, here[Y], here[X]))))

    pl.semaphore_wait(barrier, group - 1 + 2 * (depth - 1))

    loads[0].wait()

    def square(i, total):
        rows = gradient[pl.ds(pl.multiple_of(i * 8, 8), 8), :]
        for j in range(tiles):
            part = rows[:, j * LANES : (j + 1) * LANES]
            total = total + part * part
        return total

    total = lax.fori_loop(0, height // 8, square, jnp.zeros((8, LANES), jnp.float32))

    def exchange(value, buffer, place, count, device_of, send_sem, recv_sem):
        buffer[place] = jnp.sum(value, axis=0, keepdims=True)

        def copy(other, slot, sem):
            return pltpu.make_async_remote_copy(
                src_ref=buffer.at[slot], dst_ref=buffer.at[slot],
                send_sem=send_sem.at[other], recv_sem=recv_sem.at[sem],
                device_id=device_of(other), device_id_type=MESH,
            )

        for other in range(count):
            @pl.when(other != place)
            def _():
                copy(other, place, place).start()

        for other in range(count):
            @pl.when(other != place)
            def _():
                copy(other, place, place).wait_send()
                copy(other, other, other).wait_recv()

        return jnp.sum(buffer[...], axis=0)

    total = exchange(
        total, plane_sums, my_place, group,
        lambda place: (place // plane, here[Z] * plane + place % plane), plane_send, plane_recv,
    )
    total = exchange(
        total, line_sums, here[Z], depth,
        lambda other: (core, chip_at((other, here[Y], here[X]))), line_send, line_recv,
    )
    squares = jnp.sum(total, axis=1, keepdims=True)
    norm_limit = jnp.full((1, 1), limit_ref[0], jnp.float32)
    clip_factor = norm_limit / jnp.maximum(jnp.sqrt(squares), norm_limit)
    one = jnp.ones((1, 1), jnp.float32)
    first_gain = one / (one - power(beta_first, step_ref[0]))
    second_gain = one / (one - power(beta_second, step_ref[0]))
    for load in loads[1:]:
        load.wait()

    def children(source, order):
        last = jnp.int32(-1)
        for i, dim in enumerate(order):
            last = jnp.where(here[dim] != source[dim], i, last)
        ways = []
        for i, dim in enumerate(order):
            for side, step in enumerate((1, -1)):
                if sizes[dim] < 2:
                    continue
                there = list(here)
                there[dim] = here[dim] + step
                inside = (there[dim] >= 0) & (there[dim] < sizes[dim])
                away = (here[dim] - source[dim]) * step > 0
                used = inside & ((last < i) | ((last == i) & away))
                ways.append((used, 2 * dim + side, chip_at(there)))
        return ways

    starts = []
    at = 0
    for order, share in PIECES:
        size = tiles * share // sum(s for _, s in PIECES)
        starts.append((at, size))
        at += size
    assert at == tiles

    def code_slice(source, column, k):
        row = (chip_at(source) % sources) * height
        start, size = starts[k]
        lane = column * width + start * LANES
        return codes.at[
            pl.ds(pl.multiple_of(row, 16), height), pl.ds(pl.multiple_of(lane, LANES), size * LANES)
        ]

    def scale_slice(source):
        row = (chip_at(source) % sources) * height
        return scales.at[pl.ds(pl.multiple_of(row, 16), height), :]

    def my_index():
        return chip % sources

    def own_copy(k, send_sem, to):
        start, size = starts[k]
        return pltpu.make_async_remote_copy(
            src_ref=mine.at[:, pl.ds(start * LANES, size * LANES)],
            dst_ref=code_slice(here, core, k),
            send_sem=send_sem, recv_sem=code_recv.at[my_index(), core, k],
            device_id=(keeper, to), device_id_type=MESH,
        )

    def own_local(k):
        start, size = starts[k]
        return pltpu.make_async_copy(
            mine.at[:, pl.ds(start * LANES, size * LANES)], code_slice(here, core, k), local_sem.at[k]
        )

    lane = lax.broadcasted_iota(jnp.int32, (1, LANES), 1)
    pick_row = lax.broadcasted_iota(jnp.int32, (LANES, LANES), 0)
    pick_column = lax.broadcasted_iota(jnp.int32, (LANES, LANES), 1)
    per_tile = LANES // BLOCK
    step_rows = next(r for r in (64, 48, 32, 16) if height % r == 0)

    def tile(i, carry):
        j, r = i // (height // step_rows), i % (height // step_rows)
        rows = pl.ds(pl.multiple_of(r * step_rows, 16), step_rows)
        where = (rows, pl.ds(pl.multiple_of(j * LANES, LANES), LANES))
        weight = master[where]
        clipped = clip_factor * gradient[where]
        moment = beta_first * first[where] + (1.0 - beta_first) * clipped
        power_moment = beta_second * second[where] + (1.0 - beta_second) * clipped * clipped
        new_first[where] = moment
        new_second[where] = power_moment
        update = moment * first_gain / (jnp.sqrt(power_moment * second_gain) + adam_eps)
        weight = weight - learn_rate * (update + decay_rate * weight)
        new_master[where] = weight
        largest = jnp.abs(weight)
        shift = BLOCK // 2
        while shift:
            ahead = pltpu.roll(largest, LANES - shift, axis=1)
            behind = pltpu.roll(largest, shift, axis=1)
            largest = jnp.maximum(largest, jnp.where((lane & shift) == 0, ahead, behind))
            shift //= 2
        scale = jnp.maximum(largest, scale_floor).astype(jnp.bfloat16)
        mine[where] = (weight / scale.astype(jnp.float32)).astype(jnp.bfloat16)
        target = (core * tiles + j) * per_tile + pick_row // BLOCK
        pick = ((pick_row % BLOCK == 0) & (pick_column == target)).astype(jnp.float32)
        wide_scales[rows, :] += jnp.dot(
            scale, pick.astype(jnp.bfloat16), preferred_element_type=jnp.float32
        )
        return carry

    wide_scales[...] = jnp.zeros_like(wide_scales)
    per = height // step_rows
    for k, (order, _) in enumerate(PIECES):
        start, size = starts[k]
        lax.fori_loop(start * per, (start + size) * per, tile, 0)
        for used, way, to in children(here, order):
            @pl.when(used)
            def _():
                own_copy(k, own_send.at[k, way], to).start()

        @pl.when(core == keeper)
        def _():
            own_local(k).start()

        @pl.when(core != keeper)
        def _():
            own_copy(k, peer_send.at[k], chip).start()

    my_scales[...] = wide_scales[...].astype(jnp.bfloat16)
    peer_scales = pltpu.make_async_remote_copy(
        src_ref=my_scales, dst_ref=their_scales, send_sem=peer_scale_send.at[0],
        recv_sem=peer_scale_recv.at[0], device_id=(peer, chip), device_id_type=MESH,
    )

    def scale_copy(source, send_sem, to):
        index = chip_at(source) % sources
        return pltpu.make_async_remote_copy(
            src_ref=scale_slice(source), dst_ref=scale_slice(source),
            send_sem=send_sem, recv_sem=scale_recv.at[index],
            device_id=(core, to), device_id_type=MESH,
        )

    @pl.when(core != keeper)
    def _():
        peer_scales.start()

    @pl.when(core == keeper)
    def _():
        peer_scales.wait_recv()
        merged = wide_scales[...] + their_scales[...].astype(jnp.float32)
        row = pl.ds(pl.multiple_of(my_index() * height, 16), height)
        scales[row, :] = merged.astype(jnp.bfloat16)
        for used, way, to in children(here, SCALE_ORDER):
            @pl.when(used)
            def _():
                scale_copy(here, own_scale_send.at[way], to).start()

    low = core * half_depth
    top = low + half_depth - 1

    def source_of(q):
        i, j = q // plane, q % plane
        inside = low + (here[Z] - low + i + depth) % half_depth
        z = jnp.where(here[Z] >= top, top - i, jnp.where(here[Z] <= low, low + i, inside))
        return (z, (here[Y] + j // wide) % high, (here[X] + j % wide) % wide)

    def code_copy(source, column, k, send_sem, to):
        index = chip_at(source) % sources
        part = code_slice(source, column, k)
        return pltpu.make_async_remote_copy(
            src_ref=part, dst_ref=part, send_sem=send_sem,
            recv_sem=code_recv.at[index, column, k],
            device_id=(core, to), device_id_type=MESH,
        )

    def drain(q):
        source = source_of(q)
        slot = q % WINDOW

        @pl.when(chip_at(source) != chip)
        def _():
            for k, (order, _) in enumerate(PIECES):
                for column in range(2):
                    for used, way, to in children(source, order):
                        @pl.when(used)
                        def _():
                            code_copy(source, column, k, pass_send.at[slot, column, k, way], to).wait_send()

            for used, way, to in children(source, SCALE_ORDER):
                @pl.when(used)
                def _():
                    scale_copy(source, pass_scale_send.at[slot, way], to).wait_send()

    def forward(q, carry):
        source = source_of(q)
        slot = q % WINDOW
        mine_too = chip_at(source) == chip
        if sources > WINDOW:
            @pl.when(q >= WINDOW)
            def _():
                drain(q - WINDOW)

        @pl.when(mine_too)
        def _():
            for k in range(len(PIECES)):
                own_local(k).wait()
                code_copy(source, peer, k, peer_send.at[k], chip).wait_recv()

        @pl.when(jnp.logical_not(mine_too))
        def _():
            for k, (order, _) in enumerate(PIECES):
                ways = children(source, order)
                for column in range(2):
                    code_copy(source, column, k, peer_send.at[k], chip).wait_recv()
                    for used, way, to in ways:
                        @pl.when(used)
                        def _():
                            code_copy(source, column, k, pass_send.at[slot, column, k, way], to).start()

            scale_copy(source, peer_scale_send.at[0], chip).wait_recv()
            for used, way, to in children(source, SCALE_ORDER):
                @pl.when(used)
                def _():
                    scale_copy(source, pass_scale_send.at[slot, way], to).start()

        return carry

    lax.fori_loop(0, sources, forward, 0)

    def drain_step(q, carry):
        drain(q)
        return carry

    lax.fori_loop(max(0, sources - WINDOW), sources, drain_step, 0)
    for k, (order, _) in enumerate(PIECES):
        for used, way, to in children(here, order):
            @pl.when(used)
            def _():
                own_copy(k, own_send.at[k, way], to).wait_send()

        @pl.when(core != keeper)
        def _():
            own_copy(k, peer_send.at[k], chip).wait_send()

    @pl.when(core != keeper)
    def _():
        peer_scales.wait_send()

    @pl.when(core == keeper)
    def _():
        for used, way, to in children(here, SCALE_ORDER):
            @pl.when(used)
            def _():
                scale_copy(here, own_scale_send.at[way], to).wait_send()


def per_device(grid, master, gradient, first_moment, second_moment, max_norm, step_count):
    height, width = master.shape
    plane = grid[1] * grid[2]
    sources = grid[0] * plane // 2
    pieces = len(PIECES)
    kept = sources * height
    state = jax.ShapeDtypeStruct(master.shape, jnp.float32)
    held = pltpu.VMEM(master.shape, jnp.float32)
    narrow = pltpu.VMEM((height, LANES), jnp.bfloat16)
    dma = pltpu.SemaphoreType.DMA
    vmem = pl.BlockSpec(memory_space=pltpu.VMEM)
    smem = pl.BlockSpec(memory_space=pltpu.SMEM)
    hbm = pl.BlockSpec(memory_space=pltpu.HBM)
    free = pl.BlockSpec(memory_space=pl.ANY)
    state_in = [
        pltpu.with_memory_space_constraint(a, pltpu.HBM)
        for a in (master, gradient, first_moment, second_moment)
    ]
    results = pl.pallas_call(
        functools.partial(kernel, grid),
        out_shape=(
            state, state, state,
            jax.ShapeDtypeStruct((kept, 2 * width), jnp.bfloat16),
            jax.ShapeDtypeStruct((kept, 2 * width // BLOCK), jnp.bfloat16),
        ),
        in_specs=[smem, smem, hbm, hbm, hbm, hbm],
        out_specs=(vmem, vmem, vmem, free, vmem),
        scratch_shapes=[
            held, held, held, held,
            pltpu.VMEM((height, width), jnp.bfloat16),
            narrow,
            pltpu.VMEM((height, LANES), jnp.float32),
            narrow,
            pltpu.VMEM((2 * plane, 1, LANES), jnp.float32),
            pltpu.VMEM((grid[0], 1, LANES), jnp.float32),
            dma((4,)),
            dma((2 * plane,)), dma((2 * plane,)), dma((grid[0],)), dma((grid[0],)),
            dma((pieces, 6)), dma((6,)), dma((pieces,)), dma((1,)), dma((1,)),
            dma((WINDOW, 2, pieces, 6)), dma((WINDOW, 6)),
            dma((sources, 2, pieces)), dma((sources,)), dma((pieces,)),
        ],
        compiler_params=pltpu.CompilerParams(
            collective_id=0, has_side_effects=True, vmem_limit_bytes=KERNEL_VMEM
        ),
    )(max_norm, step_count, *state_in)
    return pl.pallas_call(
        flush,
        out_shape=tuple(jax.ShapeDtypeStruct(r.shape, r.dtype) for r in results),
        in_specs=[free] * len(results),
        out_specs=(hbm,) * len(results),
        scratch_shapes=[dma((len(results), PARTS))],
        compiler_params=pltpu.CompilerParams(vmem_limit_bytes=FLUSH_VMEM),
    )(*results)


def flush(*refs):
    count = len(refs) // 2
    sem = refs[-1]
    copies = []
    for i, (held, out) in enumerate(zip(refs[:count], refs[count:-1])):
        rows = held.shape[0] // PARTS
        for part in range(PARTS):
            span = pl.ds(part * rows, rows)
            copies.append(pltpu.make_async_copy(held.at[span], out.at[span], sem.at[i, part]))
    for copy in copies:
        copy.start()
    for copy in copies:
        copy.wait()


PARTS = 2
FLUSH_VMEM = 1024 * 1024


KERNEL_VMEM = 16 * 1024 * 1024


def solution(mesh):
    return jax.shard_map(
        functools.partial(per_device, grid_of(mesh)),
        mesh=mesh,
        in_specs=(
            P("shard", "pair"),
            P("shard", "pair"),
            P("shard", "pair"),
            P("shard", "pair"),
            P(),
            P(),
        ),
        out_specs=(
            P("shard", "pair"),
            P("shard", "pair"),
            P("shard", "pair"),
            P("pair", None),
            P("pair", None),
        ),
        check_vma=False,
    )
```

profile of v0, /device:TPU:1, one launch (start us, length us, event | category | flops | bytes accessed | tf_op | source)
XLA Modules:
  0.0 131.9 jit_solution(14862969422361297502)
XLA Ops:
  1.9 123.8 %shard_map.101 = (f32[192,2048]{1,0:T(8,128)S(1)}, f32[192,2048]{1,0:T(8,128)S(1)}, f32[192,2048]{1,0:T(8,128)S(1)}, bf16[1536,4096]{1,0:T(8,128)(2,1)S(1)}, bf16[1536,128]{1,0:T(8,128)(2,1)S(1)}) custom-call(f32[1]{0:T(128)S(6)} %copy.11.limit_ref, s32[1]{0:T(128)S(6)} %copy.12.step_ref, f32[192,2048]{1,0:T(8,128)} %master_hbm.1, f32[192,2048]{1,0:T(8,128)} %gradient_hbm.1, ...), custom_call_target="tpu_custom_call" | custom-call | tf_op jit(solution)/shard_map/pallas_call | solution.py:408
  125.7 6.2 %shard_map.102 = (f32[192,2048]{1,0:T(8,128)}, f32[192,2048]{1,0:T(8,128)}, f32[192,2048]{1,0:T(8,128)}, bf16[1536,4096]{1,0:T(8,128)(2,1)}, bf16[1536,128]{1,0:T(8,128)(2,1)}) custom-call(f32[192,2048]{1,0:T(8,128)S(1)} %get-tuple-element.10.refs_0_, f32[192,2048]{1,0:T(8,128)S(1)} %get-tuple-element.11.refs_1_, f32[192,2048]{1,0:T(8,128)S(1)} %get-tuple-element.12.refs_2_, ...), custom_call_target="tpu_custom_call" | custom-call | tf_op jit(solution)/shard_map/pallas_call | solution.py:435
where the time goes:
time: 132 us
  Pallas kernels  130 us (98%)
  between operations  1.93 us (1%)
    pallas_call x1, Pallas kernels, per_device(): pl.pallas_call(functools.partial(kernel, grid), out_shape=(state, state,...  124 us
    pallas_call x1, Pallas kernels, per_device(): pl.pallas_call(flush, out_shape=tuple((jax.ShapeDtypeStruct(r.shape, r.dt...  6.24 us

commit v1 on v0

v1 whole, which is shorter than its diff:
```python
import functools

import jax
import jax.numpy as jnp
from jax import lax
from jax.experimental import pallas as pl
from jax.experimental.pallas import tpu as pltpu
from jax.sharding import PartitionSpec as P

BLOCK = 32
LANES = 128

beta_first = 0.9
beta_second = 0.99
learn_rate = 0.01
decay_rate = 0.1
adam_eps = 1e-06
scale_floor = 0.25

MESH = pl.DeviceIdType.MESH
Z, Y, X = 0, 1, 2
PIECES = (
    ((Z, X, Y), (3, 3)),
    ((Z, Y, X), (3, 3)),
    ((X, Y, Z), (2, 1)),
    ((Z, X, Y), (3, 3)),
    ((Z, Y, X), (3, 4)),
    ((Y, X, Z), (2, 2)),
)
SCALE_ORDER = (Z, X, Y)


def grid_of(mesh):
    count = mesh.shape["shard"]
    at = [d.coords for d in mesh.devices.reshape(mesh.shape["pair"], count)[0]]
    sizes = tuple(len({c[d] for c in at}) for d in (2, 1, 0))
    return sizes


def power(base, exponent):
    result = jnp.float32(1.0)
    for bit in range(31):
        factor = jnp.float32(base ** (2**bit))
        result = jnp.where((exponent >> bit) & 1 == 1, result * factor, result)
    return result


def kernel(
    grid, limit_ref, step_ref, master_hbm, gradient_hbm, first_hbm, second_hbm,
    new_master, new_first, new_second, codes, scales,
    master, gradient, first, second, mine, my_scales, wide_scales, their_scales,
    plane_sums, line_sums,
    load_sem, sum_send, plane_recv, line_recv, send_sem, peer_scale_recv, recv_sem, local_sem,
):
    sizes = grid
    depth, high, wide = sizes
    plane = high * wide
    half_depth = depth // 2
    sources = half_depth * plane
    height, width = mine.shape
    tiles = width // LANES
    pieces = len(PIECES)
    core = lax.axis_index("pair")
    chip = lax.axis_index("shard")
    here = (chip // plane, (chip // wide) % high, chip % wide)
    keeper = here[Z] // half_depth
    peer = 1 - core

    def chip_at(at):
        return (at[Z] * high + at[Y]) * wide + at[X]

    def wait_bytes(ref, sem):
        pltpu.make_async_copy(ref, ref, sem).wait()

    loads = [
        pltpu.make_async_copy(source, held, load_sem.at[i])
        for i, (source, held) in enumerate(
            ((gradient_hbm, gradient), (master_hbm, master), (first_hbm, first), (second_hbm, second))
        )
    ]
    loads[0].start()

    barrier = pltpu.get_barrier_semaphore()
    group = 2 * plane
    my_place = core * plane + here[Y] * wide + here[X]

    def greet(device):
        pl.semaphore_signal(barrier, inc=1, device_id=device, device_id_type=MESH)

    for other in range(depth):
        @pl.when(other != here[Z])
        def _():
            for side in range(2):
                greet((side, chip_at((other, here[Y], here[X]))))

    for place in range(group):
        @pl.when(place != my_place)
        def _():
            greet((place // plane, here[Z] * plane + place % plane))

    for load in loads[1:]:
        load.start()
    loads[0].wait()

    def square(i, totals):
        rows = gradient[pl.ds(pl.multiple_of(i * 8, 8), 8), :]
        totals = list(totals)
        for j in range(tiles):
            part = rows[:, j * LANES : (j + 1) * LANES]
            totals[j % 4] = totals[j % 4] + part * part
        return tuple(totals)

    totals = lax.fori_loop(
        0, height // 8, square, tuple(jnp.zeros((8, LANES), jnp.float32) for _ in range(4))
    )
    total = (totals[0] + totals[1]) + (totals[2] + totals[3])
    total = jnp.sum(total, axis=0, keepdims=True)

    pl.semaphore_wait(barrier, group - 1 + 2 * (depth - 1))

    def exchange(value, buffer, place, count, device_of, recv):
        buffer[place] = value

        def copy(other):
            return pltpu.make_async_remote_copy(
                src_ref=buffer.at[place], dst_ref=buffer.at[place],
                send_sem=sum_send, recv_sem=recv,
                device_id=device_of(other), device_id_type=MESH,
            )

        for other in range(count):
            @pl.when(other != place)
            def _():
                copy(other).start()

        others = buffer.at[pl.ds(0, count - 1)]
        wait_bytes(others, recv)
        wait_bytes(others, sum_send)
        return jnp.sum(buffer[...], axis=0)

    total = exchange(
        total, plane_sums, my_place, group,
        lambda place: (place // plane, here[Z] * plane + place % plane), plane_recv,
    )
    total = exchange(
        total, line_sums, here[Z], depth,
        lambda other: (core, chip_at((other, here[Y], here[X]))), line_recv,
    )
    squares = jnp.sum(total, axis=1, keepdims=True)
    norm_limit = jnp.full((1, 1), limit_ref[0], jnp.float32)
    clip_factor = norm_limit / jnp.maximum(jnp.sqrt(squares), norm_limit)
    one = jnp.ones((1, 1), jnp.float32)
    first_gain = one / (one - power(beta_first, step_ref[0]))
    second_gain = one / (one - power(beta_second, step_ref[0]))
    clip_first = ((1.0 - beta_first) * clip_factor)[0, 0]
    clip_second = ((1.0 - beta_second) * clip_factor * clip_factor)[0, 0]
    step_gain = (learn_rate * first_gain)[0, 0]
    second_gain = second_gain[0, 0]
    for load in loads[1:]:
        load.wait()

    def children(source, order):
        last = jnp.int32(-1)
        for i, dim in enumerate(order):
            last = jnp.where(here[dim] != source[dim], i, last)
        ways = []
        for i, dim in enumerate(order):
            if sizes[dim] == 2:
                there = list(here)
                there[dim] = 1 - here[dim]
                ways.append((last < i, chip_at(there)))
            elif sizes[dim] > 2:
                for step in (1, -1):
                    there = list(here)
                    there[dim] = here[dim] + step
                    inside = (there[dim] >= 0) & (there[dim] < sizes[dim])
                    away = (here[dim] - source[dim]) * step > 0
                    ways.append((inside & ((last < i) | ((last == i) & away)), chip_at(there)))
        return ways

    spans = []
    at = [0, 0]
    for _, shares in PIECES:
        sized = [tiles * share // 16 for share in shares]
        spans.append([(at[c], sized[c]) for c in range(2)])
        at = [at[c] + sized[c] for c in range(2)]
    assert at == [tiles, tiles]

    def code_slice(source, column, k):
        row = (chip_at(source) % sources) * height
        start, size = spans[k][column]
        lane = column * width + start * LANES
        return codes.at[pl.ds(pl.multiple_of(row, 16), height), pl.ds(lane, size * LANES)]

    def scale_slice(source):
        row = (chip_at(source) % sources) * height
        return scales.at[pl.ds(pl.multiple_of(row, 16), height), :]

    def tile_block(count):
        return codes.at[pl.ds(0, height), pl.ds(0, count * LANES)]

    my_index = chip % sources

    def own_slice(column, k):
        start, size = spans[k][column]
        return mine.at[:, pl.ds(start * LANES, size * LANES)]

    def own_copy(column, k, to):
        return pltpu.make_async_remote_copy(
            src_ref=own_slice(column, k), dst_ref=code_slice(here, column, k),
            send_sem=send_sem, recv_sem=recv_sem.at[my_index, k],
            device_id=(keeper, to), device_id_type=MESH,
        )

    lane = lax.broadcasted_iota(jnp.int32, (1, LANES), 1)
    spread_row = lax.broadcasted_iota(jnp.int32, (LANES, LANES), 0)
    spread_column = lax.broadcasted_iota(jnp.int32, (LANES, LANES), 1)
    spread = (spread_row == spread_column // BLOCK * BLOCK).astype(jnp.float32).astype(jnp.bfloat16)
    per_tile = LANES // BLOCK
    assert tiles <= BLOCK

    def tile(j, carry):
        where = (slice(None), pl.ds(pl.multiple_of(j * LANES, LANES), LANES))
        weight = master[where]
        slope = gradient[where]
        moment = beta_first * first[where] + clip_first * slope
        power_moment = beta_second * second[where] + clip_second * (slope * slope)
        new_first[where] = moment
        new_second[where] = power_moment
        scaled = power_moment * second_gain
        root = scaled * lax.rsqrt(scaled)
        weight = (1.0 - learn_rate * decay_rate) * weight - step_gain * moment / (root + adam_eps)
        new_master[where] = weight
        largest = jnp.abs(weight)
        shift = BLOCK // 2
        while shift:
            largest = jnp.maximum(largest, pltpu.roll(largest, LANES - shift, axis=1))
            shift //= 2
        scale = jnp.maximum(largest, scale_floor).astype(jnp.bfloat16)
        scale = jnp.dot(scale, spread, preferred_element_type=jnp.float32)
        mine[where] = (weight / scale).astype(jnp.bfloat16)
        wide_scales[...] = jnp.where(lane % BLOCK == j, scale, wide_scales[...])
        return carry

    wide_scales[...] = jnp.zeros_like(wide_scales)
    sent = jnp.int32(0)
    for c in range(2):
        def own_pieces(sent):
            for k, (order, _) in enumerate(PIECES):
                start, size = spans[k][c]
                lax.fori_loop(start, start + size, tile, 0)
                for used, to in children(here, order):
                    @pl.when(used)
                    def _():
                        own_copy(c, k, to).start()

                    sent = sent + jnp.where(used, size, 0)

                @pl.when(c == keeper)
                def _():
                    pltpu.make_async_copy(
                        own_slice(c, k), code_slice(here, c, k), local_sem
                    ).start()

                @pl.when(c != keeper)
                def _():
                    own_copy(c, k, chip).start()

                sent = sent + jnp.where(c != keeper, size, 0)
            return sent

        sent = lax.cond(core == c, own_pieces, lambda s: s, sent)

    place_row = spread_row % BLOCK
    target = (core * tiles + place_row) * per_tile + spread_row // BLOCK
    pick = ((place_row < tiles) & (spread_column == target)).astype(jnp.float32)
    placed = jnp.dot(
        wide_scales[...].astype(jnp.bfloat16), pick.astype(jnp.bfloat16),
        preferred_element_type=jnp.float32,
    )
    my_scales[...] = placed.astype(jnp.bfloat16)
    peer_scales = pltpu.make_async_remote_copy(
        src_ref=my_scales, dst_ref=their_scales, send_sem=send_sem,
        recv_sem=peer_scale_recv, device_id=(peer, chip), device_id_type=MESH,
    )

    def scale_copy(source, to):
        return pltpu.make_async_remote_copy(
            src_ref=scale_slice(source), dst_ref=scale_slice(source),
            send_sem=send_sem, recv_sem=recv_sem.at[chip_at(source) % sources, pieces],
            device_id=(core, to), device_id_type=MESH,
        )

    @pl.when(core != keeper)
    def _():
        peer_scales.start()

    @pl.when(core == keeper)
    def _():
        peer_scales.wait_recv()
        merged = my_scales[...] + their_scales[...]
        row = pl.ds(pl.multiple_of(my_index * height, 16), height)
        scales[row, :] = merged
        for used, to in children(here, SCALE_ORDER):
            @pl.when(used)
            def _():
                scale_copy(here, to).start()

    sent = sent + jnp.where(core != keeper, 1, 0)
    for used, _ in children(here, SCALE_ORDER):
        sent = sent + jnp.where((core == keeper) & used, 1, 0)

    low = core * half_depth
    top = low + half_depth - 1

    def source_of(q):
        i, j = q // plane, q % plane
        inside = low + (here[Z] - low + i + depth) % half_depth
        z = jnp.where(here[Z] >= top, top - i, jnp.where(here[Z] <= low, low + i, inside))
        return (z, (here[Y] + j // wide) % high, (here[X] + j % wide) % wide)

    def code_copy(source, column, k, to):
        part = code_slice(source, column, k)
        return pltpu.make_async_remote_copy(
            src_ref=part, dst_ref=part, send_sem=send_sem,
            recv_sem=recv_sem.at[chip_at(source) % sources, k],
            device_id=(core, to), device_id_type=MESH,
        )

    def item_of(t):
        return t // (pieces + 1), t % (pieces + 1)

    def forward(t, sent):
        q, which = item_of(t)
        source = source_of(q)
        index = chip_at(source) % sources
        mine_too = chip_at(source) == chip

        for k, (order, _) in enumerate(PIECES):
            both = spans[k][0][1] + spans[k][1][1]

            for c in range(2):
                @pl.when((which == k) & mine_too & (core == c))
                def _():
                    wait_bytes(code_slice(source, 1 - c, k), recv_sem.at[index, k])

            for_k = (which == k) & jnp.logical_not(mine_too)
            ways = children(source, order)

            @pl.when(for_k)
            def _():
                wait_bytes(tile_block(both), recv_sem.at[index, k])
                for used, to in ways:
                    @pl.when(used)
                    def _():
                        for column in range(2):
                            code_copy(source, column, k, to).start()

            for used, _ in ways:
                sent = sent + jnp.where(for_k & used, both, 0)

        for_scale = (which == pieces) & jnp.logical_not(mine_too)
        ways = children(source, SCALE_ORDER)

        @pl.when(for_scale)
        def _():
            wait_bytes(scale_slice(source), recv_sem.at[index, pieces])
            for used, to in ways:
                @pl.when(used)
                def _():
                    scale_copy(source, to).start()

        for used, _ in ways:
            sent = sent + jnp.where(for_scale & used, 1, 0)
        return sent

    sent = lax.fori_loop(0, sources * (pieces + 1), forward, sent)

    @pl.when(core == keeper)
    def _():
        wait_bytes(mine, local_sem)

    most = 1
    while 2 * most <= 2 * tiles:
        most *= 2

    def drain(i, carry):
        wait_bytes(tile_block(most), send_sem)
        return carry

    lax.fori_loop(0, sent // most, drain, 0)
    part = most // 2
    while part:
        @pl.when((sent // part) % 2 == 1)
        def _():
            wait_bytes(tile_block(part), send_sem)

        part //= 2


def per_device(grid, master, gradient, first_moment, second_moment, max_norm, step_count):
    height, width = master.shape
    plane = grid[1] * grid[2]
    sources = grid[0] * plane // 2
    pieces = len(PIECES)
    kept = sources * height
    state = jax.ShapeDtypeStruct(master.shape, jnp.float32)
    held = pltpu.VMEM(master.shape, jnp.float32)
    narrow = pltpu.VMEM((height, LANES), jnp.bfloat16)
    dma = pltpu.SemaphoreType.DMA
    vmem = pl.BlockSpec(memory_space=pltpu.VMEM)
    smem = pl.BlockSpec(memory_space=pltpu.SMEM)
    hbm = pl.BlockSpec(memory_space=pltpu.HBM)
    free = pl.BlockSpec(memory_space=pl.ANY)
    state_in = [
        pltpu.with_memory_space_constraint(a, pltpu.HBM)
        for a in (master, gradient, first_moment, second_moment)
    ]
    results = pl.pallas_call(
        functools.partial(kernel, grid),
        out_shape=(
            state, state, state,
            jax.ShapeDtypeStruct((kept, 2 * width), jnp.bfloat16),
            jax.ShapeDtypeStruct((kept, 2 * width // BLOCK), jnp.bfloat16),
        ),
        in_specs=[smem, smem, hbm, hbm, hbm, hbm],
        out_specs=(vmem, vmem, vmem, free, vmem),
        scratch_shapes=[
            held, held, held, held,
            pltpu.VMEM((height, width), jnp.bfloat16),
            narrow,
            pltpu.VMEM((height, LANES), jnp.float32),
            narrow,
            pltpu.VMEM((2 * plane, 1, LANES), jnp.float32),
            pltpu.VMEM((grid[0], 1, LANES), jnp.float32),
            dma((4,)), dma(()), dma(()), dma(()), dma(()), dma(()),
            dma((sources, pieces + 1)), dma(()),
        ],
        compiler_params=pltpu.CompilerParams(
            collective_id=0, has_side_effects=True, vmem_limit_bytes=KERNEL_VMEM
        ),
    )(max_norm, step_count, *state_in)
    return pl.pallas_call(
        flush,
        out_shape=tuple(jax.ShapeDtypeStruct(r.shape, r.dtype) for r in results),
        in_specs=[free] * len(results),
        out_specs=(hbm,) * len(results),
        scratch_shapes=[dma((len(results), PARTS))],
        compiler_params=pltpu.CompilerParams(vmem_limit_bytes=FLUSH_VMEM),
    )(*results)


def flush(*refs):
    count = len(refs) // 2
    sem = refs[-1]
    copies = []
    for i, (held, out) in enumerate(zip(refs[:count], refs[count:-1])):
        rows = held.shape[0] // PARTS
        for part in range(PARTS):
            span = pl.ds(part * rows, rows)
            copies.append(pltpu.make_async_copy(held.at[span], out.at[span], sem.at[i, part]))
    for copy in copies:
        copy.start()
    for copy in copies:
        copy.wait()


PARTS = 2
FLUSH_VMEM = 1024 * 1024


KERNEL_VMEM = 16 * 1024 * 1024


def solution(mesh):
    return jax.shard_map(
        functools.partial(per_device, grid_of(mesh)),
        mesh=mesh,
        in_specs=(
            P("shard", "pair"),
            P("shard", "pair"),
            P("shard", "pair"),
            P("shard", "pair"),
            P(),
            P(),
        ),
        out_specs=(
            P("shard", "pair"),
            P("shard", "pair"),
            P("shard", "pair"),
            P("pair", None),
            P("pair", None),
        ),
        check_vma=False,
    )
```

time: 132 us -> 118 us (0.89)
  Pallas kernels: 130 us -> 116 us
    pallas_call x1, Pallas kernels: 124 us -> 110 us  [per_device(): pl.pallas_call(functools.partial(kernel, grid), out_shape=(state, state,...]
where the time goes in v1:
time: 118 us
  Pallas kernels  116 us (98%)
  between operations  1.93 us (2%)
    pallas_call x1, Pallas kernels, per_device(): pl.pallas_call(functools.partial(kernel, grid), out_shape=(state, state,...  110 us
    pallas_call x1, Pallas kernels, per_device(): pl.pallas_call(flush, out_shape=tuple((jax.ShapeDtypeStruct(r.shape, r.dt...  6.24 us

profile of v1, /device:TPU:1, one launch (start us, length us, event | category | flops | bytes accessed | tf_op | source)
XLA Modules:
  0.0 117.8 jit_solution(14414482099689796037)
XLA Ops:
  1.9 109.7 %shard_map.101 = (f32[192,2048]{1,0:T(8,128)S(1)}, f32[192,2048]{1,0:T(8,128)S(1)}, f32[192,2048]{1,0:T(8,128)S(1)}, bf16[1536,4096]{1,0:T(8,128)(2,1)S(1)}, bf16[1536,128]{1,0:T(8,128)(2,1)S(1)}) custom-call(f32[1]{0:T(128)S(6)} %copy.11.limit_ref, s32[1]{0:T(128)S(6)} %copy.12.step_ref, f32[192,2048]{1,0:T(8,128)} %master_hbm.1, f32[192,2048]{1,0:T(8,128)} %gradient_hbm.1, ...), custom_call_target="tpu_custom_call" | custom-call | tf_op jit(solution)/shard_map/pallas_call | solution.py:419
  111.6 6.2 %shard_map.102 = (f32[192,2048]{1,0:T(8,128)}, f32[192,2048]{1,0:T(8,128)}, f32[192,2048]{1,0:T(8,128)}, bf16[1536,4096]{1,0:T(8,128)(2,1)}, bf16[1536,128]{1,0:T(8,128)(2,1)}) custom-call(f32[192,2048]{1,0:T(8,128)S(1)} %get-tuple-element.10.refs_0_, f32[192,2048]{1,0:T(8,128)S(1)} %get-tuple-element.11.refs_1_, f32[192,2048]{1,0:T(8,128)S(1)} %get-tuple-element.12.refs_2_, ...), custom_call_target="tpu_custom_call" | custom-call | tf_op jit(solution)/shard_map/pallas_call | solution.py:443

commit v2 on v1

--- a/solution.py
+++ b/solution.py
@@ -20,14 +20,30 @@
 MESH = pl.DeviceIdType.MESH
 Z, Y, X = 0, 1, 2
 PIECES = (
-    ((Z, X, Y), (3, 3)),
-    ((Z, Y, X), (3, 3)),
-    ((X, Y, Z), (2, 1)),
-    ((Z, X, Y), (3, 3)),
-    ((Z, Y, X), (3, 4)),
-    ((Y, X, Z), (2, 2)),
+    ((Z, X, Y), 0, 4),
+    ((Z, Y, X), 1, 4),
+    ((Y, X, Z), 0, 4),
+    ((X, Y, Z), 1, 3),
+    ((Z, Y, X), 0, 4),
+    ((Z, X, Y), 1, 4),
+    ((Z, X, Y), 0, 4),
+    ((Z, Y, X), 1, 5),
 )
 SCALE_ORDER = (Z, X, Y)
+ITEMS = {
+    (4, 2, 2): (
+        (0, 2), (0, 5), (0, 0), (0, 8), (0, 7), (0, 6), (0, 3), (0, 1), (0, 4), (2, 2),
+        (1, 0), (4, 1), (2, 0), (1, 1), (2, 5), (1, 2), (1, 7), (2, 4), (4, 0), (1, 4),
+        (4, 6), (4, 2), (1, 8), (1, 6), (2, 1), (2, 7), (1, 3), (3, 3), (5, 0), (6, 0),
+        (2, 3), (4, 4), (4, 5), (4, 7), (4, 3), (6, 1), (1, 5), (3, 8), (2, 8), (3, 0),
+        (6, 2), (3, 7), (7, 0), (2, 6), (7, 3), (3, 2), (4, 8), (6, 3), (6, 4), (6, 5),
+        (3, 1), (5, 1), (5, 5), (5, 2), (5, 4), (5, 6), (6, 7), (3, 6), (7, 2), (6, 8),
+        (5, 8), (5, 7), (6, 6), (5, 3), (7, 4), (3, 4), (3, 5), (7, 6), (7, 1), (7, 5),
+        (7, 8), (7, 7),
+    ),
+}
+WORD = 4
+ONE_STAGE = 32
 
 
 def grid_of(mesh):
@@ -49,8 +65,8 @@
     grid, limit_ref, step_ref, master_hbm, gradient_hbm, first_hbm, second_hbm,
     new_master, new_first, new_second, codes, scales,
     master, gradient, first, second, mine, my_scales, wide_scales, their_scales,
-    plane_sums, line_sums,
-    load_sem, sum_send, plane_recv, line_recv, send_sem, peer_scale_recv, recv_sem, local_sem,
+    group_sums, line_sums,
+    load_sem, sum_send, group_recv, line_recv, send_sem, peer_scale_recv, recv_sem, local_sem,
 ):
     sizes = grid
     depth, high, wide = sizes
@@ -79,24 +95,41 @@
         )
     ]
     loads[0].start()
-
     barrier = pltpu.get_barrier_semaphore()
-    group = 2 * plane
-    my_place = core * plane + here[Y] * wide + here[X]
+    chips = depth * plane
+    one_stage = 2 * chips <= ONE_STAGE
+    if one_stage:
+        group = 2 * chips
+        my_place = core * chips + chip
+    else:
+        group = 2 * plane
+        my_place = core * plane + here[Y] * wide + here[X]
+
+    def member(place):
+        if one_stage:
+            return (place // chips, place % chips)
+        return (place // plane, here[Z] * plane + place % plane)
 
     def greet(device):
         pl.semaphore_signal(barrier, inc=1, device_id=device, device_id_type=MESH)
 
-    for other in range(depth):
-        @pl.when(other != here[Z])
-        def _():
-            for side in range(2):
-                greet((side, chip_at((other, here[Y], here[X]))))
-
-    for place in range(group):
+    def greet_member(place, carry):
         @pl.when(place != my_place)
         def _():
-            greet((place // plane, here[Z] * plane + place % plane))
+            greet(member(place))
+
+        return carry
+
+    lax.fori_loop(0, group, greet_member, 0)
+    greeted = group - 1
+    if not one_stage:
+        for other in range(depth):
+            @pl.when(other != here[Z])
+            def _():
+                for side in range(2):
+                    greet((side, chip_at((other, here[Y], here[X]))))
+
+        greeted += 2 * (depth - 1)
 
     for load in loads[1:]:
         load.start()
@@ -116,7 +149,14 @@
     total = (totals[0] + totals[1]) + (totals[2] + totals[3])
     total = jnp.sum(total, axis=0, keepdims=True)
 
-    pl.semaphore_wait(barrier, group - 1 + 2 * (depth - 1))
+    one = jnp.ones((1, 1), jnp.float32)
+    first_gain = one / (one - power(beta_first, step_ref[0]))
+    second_gain = one / (one - power(beta_second, step_ref[0]))
+    step_gain = jnp.broadcast_to(learn_rate * first_gain, (1, LANES))
+    second_gain = jnp.broadcast_to(second_gain, (1, LANES))
+    norm_limit = jnp.full((1, 1), limit_ref[0], jnp.float32)
+
+    pl.semaphore_wait(barrier, greeted)
 
     def exchange(value, buffer, place, count, device_of, recv):
         buffer[place] = value
@@ -128,34 +168,30 @@
                 device_id=device_of(other), device_id_type=MESH,
             )
 
-        for other in range(count):
+        def send(other, carry):
             @pl.when(other != place)
             def _():
                 copy(other).start()
 
+            return carry
+
+        lax.fori_loop(0, count, send, 0)
         others = buffer.at[pl.ds(0, count - 1)]
         wait_bytes(others, recv)
         wait_bytes(others, sum_send)
-        return jnp.sum(buffer[...], axis=0)
-
-    total = exchange(
-        total, plane_sums, my_place, group,
-        lambda place: (place // plane, here[Z] * plane + place % plane), plane_recv,
-    )
-    total = exchange(
-        total, line_sums, here[Z], depth,
-        lambda other: (core, chip_at((other, here[Y], here[X]))), line_recv,
-    )
+        return jnp.sum(buffer[pl.ds(0, count)], axis=0)
+
+    total = exchange(total, group_sums, my_place, group, member, group_recv)
+    if not one_stage:
+        total = exchange(
+            total, line_sums, here[Z], depth,
+            lambda other: (core, chip_at((other, here[Y], here[X]))), line_recv,
+        )
     squares = jnp.sum(total, axis=1, keepdims=True)
-    norm_limit = jnp.full((1, 1), limit_ref[0], jnp.float32)
     clip_factor = norm_limit / jnp.maximum(jnp.sqrt(squares), norm_limit)
-    one = jnp.ones((1, 1), jnp.float32)
-    first_gain = one / (one - power(beta_first, step_ref[0]))
-    second_gain = one / (one - power(beta_second, step_ref[0]))
-    clip_first = ((1.0 - beta_first) * clip_factor)[0, 0]
-    clip_second = ((1.0 - beta_second) * clip_factor * clip_factor)[0, 0]
-    step_gain = (learn_rate * first_gain)[0, 0]
-    second_gain = second_gain[0, 0]
+    clip_factor = jnp.broadcast_to(clip_factor, (1, LANES))
+    clip_first = (1.0 - beta_first) * clip_factor
+    clip_second = (1.0 - beta_second) * clip_factor * clip_factor
     for load in loads[1:]:
         load.wait()
 
@@ -180,17 +216,18 @@
 
     spans = []
     at = [0, 0]
-    for _, shares in PIECES:
-        sized = [tiles * share // 16 for share in shares]
-        spans.append([(at[c], sized[c]) for c in range(2)])
-        at = [at[c] + sized[c] for c in range(2)]
+    for _, column, share in PIECES:
+        spans.append((at[column], tiles * share // 16))
+        at[column] += spans[-1][1]
     assert at == [tiles, tiles]
 
-    def code_slice(source, column, k):
+    def code_part(source, column, start, size):
         row = (chip_at(source) % sources) * height
-        start, size = spans[k][column]
         lane = column * width + start * LANES
         return codes.at[pl.ds(pl.multiple_of(row, 16), height), pl.ds(lane, size * LANES)]
+
+    def code_slice(source, k):
+        return code_part(source, PIECES[k][1], *spans[k])
 
     def scale_slice(source):
         row = (chip_at(source) % sources) * height
@@ -201,13 +238,12 @@
 
     my_index = chip % sources
 
-    def own_slice(column, k):
-        start, size = spans[k][column]
+    def own_slice(start, size):
         return mine.at[:, pl.ds(start * LANES, size * LANES)]
 
-    def own_copy(column, k, to):
+    def own_copy(column, k, start, size, to):
         return pltpu.make_async_remote_copy(
-            src_ref=own_slice(column, k), dst_ref=code_slice(here, column, k),
+            src_ref=own_slice(start, size), dst_ref=code_part(here, column, start, size),
             send_sem=send_sem, recv_sem=recv_sem.at[my_index, k],
             device_id=(keeper, to), device_id_type=MESH,
         )
@@ -246,27 +282,32 @@
     sent = jnp.int32(0)
     for c in range(2):
         def own_pieces(sent):
-            for k, (order, _) in enumerate(PIECES):
-                start, size = spans[k][c]
-                lax.fori_loop(start, start + size, tile, 0)
-                for used, to in children(here, order):
-                    @pl.when(used)
+            for k, (order, column, _) in enumerate(PIECES):
+                if column != c:
+                    continue
+                start, size = spans[k]
+                parts = ((0, 1), (1, size - 1)) if start == 0 and size > 1 else ((0, size),)
+                for offset, part in parts:
+                    begin = start + offset
+                    lax.fori_loop(begin, begin + part, tile, 0)
+                    for used, to in children(here, order):
+                        @pl.when(used)
+                        def _():
+                            own_copy(c, k, begin, part, to).start()
+
+                        sent = sent + jnp.where(used, part, 0)
+
+                    @pl.when(c == keeper)
                     def _():
-                        own_copy(c, k, to).start()
-
-                    sent = sent + jnp.where(used, size, 0)
-
-                @pl.when(c == keeper)
-                def _():
-                    pltpu.make_async_copy(
-                        own_slice(c, k), code_slice(here, c, k), local_sem
-                    ).start()
-
-                @pl.when(c != keeper)
-                def _():
-                    own_copy(c, k, chip).start()
-
-                sent = sent + jnp.where(c != keeper, size, 0)
+                        pltpu.make_async_copy(
+                            own_slice(begin, part), code_part(here, c, begin, part), local_sem
+                        ).start()
+
+                    @pl.when(c != keeper)
+                    def _():
+                        own_copy(c, k, begin, part, chip).start()
+
+                    sent = sent + jnp.where(c != keeper, part, 0)
             return sent
 
         sent = lax.cond(core == c, own_pieces, lambda s: s, sent)
@@ -319,16 +360,30 @@
         z = jnp.where(here[Z] >= top, top - i, jnp.where(here[Z] <= low, low + i, inside))
         return (z, (here[Y] + j // wide) % high, (here[X] + j % wide) % wide)
 
-    def code_copy(source, column, k, to):
-        part = code_slice(source, column, k)
+    def code_copy(source, k, to):
+        part = code_slice(source, k)
         return pltpu.make_async_remote_copy(
             src_ref=part, dst_ref=part, send_sem=send_sem,
             recv_sem=recv_sem.at[chip_at(source) % sources, k],
             device_id=(core, to), device_id_type=MESH,
         )
 
+    items = ITEMS.get(sizes)
+    words = []
+    if items:
+        assert sorted(items) == [(q, k) for q in range(sources) for k in range(pieces + 1)]
+        for start in range(0, len(items), WORD):
+            chunk = items[start : start + WORD]
+            words.append(sum((16 * q + k) << (7 * i) for i, (q, k) in enumerate(chunk)))
+
     def item_of(t):
-        return t // (pieces + 1), t % (pieces + 1)
+        if not words:
+            return t // (pieces + 1), t % (pieces + 1)
+        word = jnp.int32(0)
+        for i, held in enumerate(words):
+            word = jnp.where(t // WORD == i, held, word)
+        item = (word >> (7 * (t % WORD))) % 128
+        return item // 16, item % 16
 
     def forward(t, sent):
         q, which = item_of(t)
@@ -336,28 +391,23 @@
         index = chip_at(source) % sources
         mine_too = chip_at(source) == chip
 
-        for k, (order, _) in enumerate(PIECES):
-            both = spans[k][0][1] + spans[k][1][1]
-
-            for c in range(2):
-                @pl.when((which == k) & mine_too & (core == c))
-                def _():
-                    wait_bytes(code_slice(source, 1 - c, k), recv_sem.at[index, k])
+        for k, (order, column, _) in enumerate(PIECES):
+            @pl.when((which == k) & jnp.logical_not(mine_too & (core == column)))
+            def _():
+                wait_bytes(code_slice(source, k), recv_sem.at[index, k])
 
             for_k = (which == k) & jnp.logical_not(mine_too)
             ways = children(source, order)
 
             @pl.when(for_k)
             def _():
-                wait_bytes(tile_block(both), recv_sem.at[index, k])
                 for used, to in ways:
                     @pl.when(used)
                     def _():
-                        for column in range(2):
-                            code_copy(source, column, k, to).start()
+                        code_copy(source, k, to).start()
 
             for used, _ in ways:
-                sent = sent + jnp.where(for_k & used, both, 0)
+                sent = sent + jnp.where(for_k & used, spans[k][1], 0)
 
         for_scale = (which == pieces) & jnp.logical_not(mine_too)
         ways = children(source, SCALE_ORDER)
@@ -431,7 +481,7 @@
             narrow,
             pltpu.VMEM((height, LANES), jnp.float32),
             narrow,
-            pltpu.VMEM((2 * plane, 1, LANES), jnp.float32),
+            pltpu.VMEM((max(2 * plane, ONE_STAGE), 1, LANES), jnp.float32),
             pltpu.VMEM((grid[0], 1, LANES), jnp.float32),
             dma((4,)), dma(()), dma(()), dma(()), dma(()), dma(()),
             dma((sources, pieces + 1)), dma(()),

time: 118 us -> 110 us (0.932)
  Pallas kernels: 116 us -> 107 us
    pallas_call x1, Pallas kernels: 110 us -> 101 us  [per_device(): pl.pallas_call(functools.partial(kernel, grid), out_shape=(state, state,...]
where the time goes in v2:
time: 110 us; the launch traced here: 109 us
  Pallas kernels  107 us (97%)
  between operations  1.93 us (2%)
    pallas_call x1, Pallas kernels, per_device(): pl.pallas_call(functools.partial(kernel, grid), out_shape=(state, state,...  101 us
    pallas_call x1, Pallas kernels, per_device(): pl.pallas_call(flush, out_shape=tuple((jax.ShapeDtypeStruct(r.shape, r.dt...  6.24 us

profile of v2, /device:TPU:1, one launch (start us, length us, event | category | flops | bytes accessed | tf_op | source)
XLA Modules:
  0.0 109.4 jit_solution(17202992754136357444)
XLA Ops:
  1.9 101.3 %shard_map.101 = (f32[192,2048]{1,0:T(8,128)S(1)}, f32[192,2048]{1,0:T(8,128)S(1)}, f32[192,2048]{1,0:T(8,128)S(1)}, bf16[1536,4096]{1,0:T(8,128)(2,1)S(1)}, bf16[1536,128]{1,0:T(8,128)(2,1)S(1)}) custom-call(f32[1]{0:T(128)S(6)} %copy.11.limit_ref, s32[1]{0:T(128)S(6)} %copy.12.step_ref, f32[192,2048]{1,0:T(8,128)} %master_hbm.1, f32[192,2048]{1,0:T(8,128)} %gradient_hbm.1, ...), custom_call_target="tpu_custom_call" | custom-call | tf_op jit(solution)/shard_map/pallas_call | solution.py:469
  103.2 6.2 %shard_map.102 = (f32[192,2048]{1,0:T(8,128)}, f32[192,2048]{1,0:T(8,128)}, f32[192,2048]{1,0:T(8,128)}, bf16[1536,4096]{1,0:T(8,128)(2,1)}, bf16[1536,128]{1,0:T(8,128)(2,1)}) custom-call(f32[192,2048]{1,0:T(8,128)S(1)} %get-tuple-element.10.refs_0_, f32[192,2048]{1,0:T(8,128)S(1)} %get-tuple-element.11.refs_1_, f32[192,2048]{1,0:T(8,128)S(1)} %get-tuple-element.12.refs_2_, ...), custom_call_target="tpu_custom_call" | custom-call | tf_op jit(solution)/shard_map/pallas_call | solution.py:493

commit v3 on v2

--- a/solution.py
+++ b/solution.py
@@ -21,25 +21,25 @@
 Z, Y, X = 0, 1, 2
 PIECES = (
     ((Z, X, Y), 0, 4),
+    ((Y, X, Z), 1, 2),
+    ((Z, Y, X), 0, 4),
     ((Z, Y, X), 1, 4),
-    ((Y, X, Z), 0, 4),
-    ((X, Y, Z), 1, 3),
-    ((Z, Y, X), 0, 4),
-    ((Z, X, Y), 1, 4),
-    ((Z, X, Y), 0, 4),
-    ((Z, Y, X), 1, 5),
+    ((X, Y, Z), 0, 5),
+    ((Z, X, Y), 1, 6),
+    ((Z, X, Y), 0, 3),
+    ((Z, Y, X), 1, 4),
 )
-SCALE_ORDER = (Z, X, Y)
+SCALE_ORDER = (Y, Z, X)
 ITEMS = {
     (4, 2, 2): (
-        (0, 2), (0, 5), (0, 0), (0, 8), (0, 7), (0, 6), (0, 3), (0, 1), (0, 4), (2, 2),
-        (1, 0), (4, 1), (2, 0), (1, 1), (2, 5), (1, 2), (1, 7), (2, 4), (4, 0), (1, 4),
-        (4, 6), (4, 2), (1, 8), (1, 6), (2, 1), (2, 7), (1, 3), (3, 3), (5, 0), (6, 0),
-        (2, 3), (4, 4), (4, 5), (4, 7), (4, 3), (6, 1), (1, 5), (3, 8), (2, 8), (3, 0),
-        (6, 2), (3, 7), (7, 0), (2, 6), (7, 3), (3, 2), (4, 8), (6, 3), (6, 4), (6, 5),
-        (3, 1), (5, 1), (5, 5), (5, 2), (5, 4), (5, 6), (6, 7), (3, 6), (7, 2), (6, 8),
-        (5, 8), (5, 7), (6, 6), (5, 3), (7, 4), (3, 4), (3, 5), (7, 6), (7, 1), (7, 5),
-        (7, 8), (7, 7),
+        (0, 3), (1, 4), (0, 6), (4, 3), (0, 0), (2, 1), (4, 5), (4, 0), (1, 1), (3, 4),
+        (4, 6), (2, 8), (0, 2), (4, 8), (1, 6), (4, 7), (2, 3), (0, 7), (6, 3), (6, 8),
+        (6, 0), (5, 0), (6, 5), (2, 6), (0, 8), (2, 0), (2, 2), (4, 1), (3, 8), (3, 1),
+        (0, 4), (0, 5), (4, 2), (1, 7), (7, 4), (1, 0), (4, 4), (1, 2), (5, 5), (5, 6),
+        (2, 4), (6, 6), (7, 1), (5, 3), (2, 7), (6, 7), (5, 4), (1, 5), (5, 8), (7, 3),
+        (6, 2), (1, 8), (6, 4), (3, 6), (1, 3), (5, 1), (0, 1), (2, 5), (3, 3), (7, 0),
+        (3, 0), (7, 8), (3, 7), (5, 7), (7, 5), (3, 2), (5, 2), (7, 6), (6, 1), (7, 7),
+        (3, 5), (7, 2),
     ),
 }
 WORD = 4

time: 110 us -> 110 us (level)
  no operation moved by 1% of the time
where the time goes in v3:
time: 110 us
  Pallas kernels  108 us (98%)
  between operations  1.93 us (2%)
    pallas_call x1, Pallas kernels, per_device(): pl.pallas_call(functools.partial(kernel, grid), out_shape=(state, state,...  101 us
    pallas_call x1, Pallas kernels, per_device(): pl.pallas_call(flush, out_shape=tuple((jax.ShapeDtypeStruct(r.shape, r.dt...  6.24 us

profile of v3, /device:TPU:1, one launch (start us, length us, event | category | flops | bytes accessed | tf_op | source)
XLA Modules:
  0.0 109.7 jit_solution(2508916027547926975)
XLA Ops:
  1.9 101.5 %shard_map.101 = (f32[192,2048]{1,0:T(8,128)S(1)}, f32[192,2048]{1,0:T(8,128)S(1)}, f32[192,2048]{1,0:T(8,128)S(1)}, bf16[1536,4096]{1,0:T(8,128)(2,1)S(1)}, bf16[1536,128]{1,0:T(8,128)(2,1)S(1)}) custom-call(f32[1]{0:T(128)S(6)} %copy.11.limit_ref, s32[1]{0:T(128)S(6)} %copy.12.step_ref, f32[192,2048]{1,0:T(8,128)} %master_hbm.1, f32[192,2048]{1,0:T(8,128)} %gradient_hbm.1, ...), custom_call_target="tpu_custom_call" | custom-call | tf_op jit(solution)/shard_map/pallas_call | solution.py:469
  103.4 6.2 %shard_map.102 = (f32[192,2048]{1,0:T(8,128)}, f32[192,2048]{1,0:T(8,128)}, f32[192,2048]{1,0:T(8,128)}, bf16[1536,4096]{1,0:T(8,128)(2,1)}, bf16[1536,128]{1,0:T(8,128)(2,1)}) custom-call(f32[192,2048]{1,0:T(8,128)S(1)} %get-tuple-element.10.refs_0_, f32[192,2048]{1,0:T(8,128)S(1)} %get-tuple-element.11.refs_1_, f32[192,2048]{1,0:T(8,128)S(1)} %get-tuple-element.12.refs_2_, ...), custom_call_target="tpu_custom_call" | custom-call | tf_op jit(solution)/shard_map/pallas_call | solution.py:493

commit v4 on v3

--- a/solution.py
+++ b/solution.py
@@ -30,6 +30,7 @@
     ((Z, Y, X), 1, 4),
 )
 SCALE_ORDER = (Y, Z, X)
+ROWS = 16
 ITEMS = {
     (4, 2, 2): (
         (0, 3), (1, 4), (0, 6), (4, 3), (0, 0), (2, 1), (4, 5), (4, 0), (1, 1), (3, 4),
@@ -221,10 +222,10 @@
         at[column] += spans[-1][1]
     assert at == [tiles, tiles]
 
-    def code_part(source, column, start, size):
-        row = (chip_at(source) % sources) * height
+    def code_part(source, column, start, size, top_row=0, rows=height):
+        row = (chip_at(source) % sources) * height + top_row
         lane = column * width + start * LANES
-        return codes.at[pl.ds(pl.multiple_of(row, 16), height), pl.ds(lane, size * LANES)]
+        return codes.at[pl.ds(pl.multiple_of(row, ROWS), rows), pl.ds(lane, size * LANES)]
 
     def code_slice(source, k):
         return code_part(source, PIECES[k][1], *spans[k])
@@ -233,17 +234,22 @@
         row = (chip_at(source) % sources) * height
         return scales.at[pl.ds(pl.multiple_of(row, 16), height), :]
 
-    def tile_block(count):
-        return codes.at[pl.ds(0, height), pl.ds(0, count * LANES)]
+    strips = height // ROWS
+    broad = 1
+    while 2 * broad <= 2 * tiles:
+        broad *= 2
+
+    def blocks(count):
+        if count <= broad:
+            return codes.at[pl.ds(0, ROWS), pl.ds(0, count * LANES)]
+        return codes.at[pl.ds(0, count // broad * ROWS), pl.ds(0, broad * LANES)]
 
     my_index = chip % sources
 
-    def own_slice(start, size):
-        return mine.at[:, pl.ds(start * LANES, size * LANES)]
-
-    def own_copy(column, k, start, size, to):
+    def own_copy(column, k, start, size, top_row, rows, to):
         return pltpu.make_async_remote_copy(
-            src_ref=own_slice(start, size), dst_ref=code_part(here, column, start, size),
+            src_ref=mine.at[pl.ds(top_row, rows), pl.ds(start * LANES, size * LANES)],
+            dst_ref=code_part(here, column, start, size, top_row, rows),
             send_sem=send_sem, recv_sem=recv_sem.at[my_index, k],
             device_id=(keeper, to), device_id_type=MESH,
         )
@@ -255,8 +261,9 @@
     per_tile = LANES // BLOCK
     assert tiles <= BLOCK
 
-    def tile(j, carry):
-        where = (slice(None), pl.ds(pl.multiple_of(j * LANES, LANES), LANES))
+    def tile(j, top_row=0, rows=height):
+        band = pl.ds(top_row, rows)
+        where = (band, pl.ds(pl.multiple_of(j * LANES, LANES), LANES))
         weight = master[where]
         slope = gradient[where]
         moment = beta_first * first[where] + clip_first * slope
@@ -275,8 +282,7 @@
         scale = jnp.maximum(largest, scale_floor).astype(jnp.bfloat16)
         scale = jnp.dot(scale, spread, preferred_element_type=jnp.float32)
         mine[where] = (weight / scale).astype(jnp.bfloat16)
-        wide_scales[...] = jnp.where(lane % BLOCK == j, scale, wide_scales[...])
-        return carry
+        wide_scales[band, :] = jnp.where(lane % BLOCK == j, scale, wide_scales[band, :])
 
     wide_scales[...] = jnp.zeros_like(wide_scales)
     sent = jnp.int32(0)
@@ -286,28 +292,33 @@
                 if column != c:
                     continue
                 start, size = spans[k]
-                parts = ((0, 1), (1, size - 1)) if start == 0 and size > 1 else ((0, size),)
-                for offset, part in parts:
+                parts = [(0, size, 0, height)]
+                if start == 0:
+                    parts = [(i, 1, 0, height) for i in range(size)]
+                    cut = strips // 2 * ROWS
+                    if cut:
+                        parts[:1] = [(0, 1, 0, cut), (0, 1, cut, height - cut)]
+                for offset, part, top_row, rows in parts:
                     begin = start + offset
-                    lax.fori_loop(begin, begin + part, tile, 0)
+
+                    def one_tile(j, carry):
+                        tile(j, top_row, rows)
+                        return carry
+
+                    lax.fori_loop(begin, begin + part, one_tile, 0)
+                    amount = part * rows // ROWS
                     for used, to in children(here, order):
                         @pl.when(used)
                         def _():
-                            own_copy(c, k, begin, part, to).start()
-
-                        sent = sent + jnp.where(used, part, 0)
-
-                    @pl.when(c == keeper)
-                    def _():
-                        pltpu.make_async_copy(
-                            own_slice(begin, part), code_part(here, c, begin, part), local_sem
-                        ).start()
+                            own_copy(c, k, begin, part, top_row, rows, to).start()
+
+                        sent = sent + jnp.where(used, amount, 0)
 
                     @pl.when(c != keeper)
                     def _():
-                        own_copy(c, k, begin, part, chip).start()
-
-                    sent = sent + jnp.where(c != keeper, part, 0)
+                        own_copy(c, k, begin, part, top_row, rows, chip).start()
+
+                    sent = sent + jnp.where(c != keeper, amount, 0)
             return sent
 
         sent = lax.cond(core == c, own_pieces, lambda s: s, sent)
@@ -347,9 +358,18 @@
             def _():
                 scale_copy(here, to).start()
 
-    sent = sent + jnp.where(core != keeper, 1, 0)
+    sent = sent + jnp.where(core != keeper, strips, 0)
     for used, _ in children(here, SCALE_ORDER):
-        sent = sent + jnp.where((core == keeper) & used, 1, 0)
+        sent = sent + jnp.where((core == keeper) & used, strips, 0)
+
+    @pl.when(core == keeper)
+    def _():
+        row = my_index * height
+        own = codes.at[
+            pl.ds(pl.multiple_of(row, ROWS), height),
+            pl.ds(pl.multiple_of(core * width, LANES), width),
+        ]
+        pltpu.make_async_copy(mine, own, local_sem).start()
 
     low = core * half_depth
     top = low + half_depth - 1
@@ -407,7 +427,7 @@
                         code_copy(source, k, to).start()
 
             for used, _ in ways:
-                sent = sent + jnp.where(for_k & used, spans[k][1], 0)
+                sent = sent + jnp.where(for_k & used, spans[k][1] * strips, 0)
 
         for_scale = (which == pieces) & jnp.logical_not(mine_too)
         ways = children(source, SCALE_ORDER)
@@ -421,7 +441,7 @@
                     scale_copy(source, to).start()
 
         for used, _ in ways:
-            sent = sent + jnp.where(for_scale & used, 1, 0)
+            sent = sent + jnp.where(for_scale & used, strips, 0)
         return sent
 
     sent = lax.fori_loop(0, sources * (pieces + 1), forward, sent)
@@ -430,12 +450,12 @@
     def _():
         wait_bytes(mine, local_sem)
 
-    most = 1
-    while 2 * most <= 2 * tiles:
+    most = broad
+    while 2 * most <= broad * (codes.shape[0] // ROWS):
         most *= 2
 
     def drain(i, carry):
-        wait_bytes(tile_block(most), send_sem)
+        wait_bytes(blocks(most), send_sem)
         return carry
 
     lax.fori_loop(0, sent // most, drain, 0)
@@ -443,7 +463,7 @@
     while part:
         @pl.when((sent // part) % 2 == 1)
         def _():
-            wait_bytes(tile_block(part), send_sem)
+            wait_bytes(blocks(part), send_sem)
 
         part //= 2
 

time: 110 us -> 109 us (level)
  no operation moved by 1% of the time
where the time goes in v4:
time: 109 us
  Pallas kernels  107 us (98%)
  between operations  1.93 us (2%)
    pallas_call x1, Pallas kernels, per_device(): pl.pallas_call(functools.partial(kernel, grid), out_shape=(state, state,...  101 us
    pallas_call x1, Pallas kernels, per_device(): pl.pallas_call(flush, out_shape=tuple((jax.ShapeDtypeStruct(r.shape, r.dt...  6.24 us

profile of v4, /device:TPU:1, one launch (start us, length us, event | category | flops | bytes accessed | tf_op | source)
XLA Modules:
  0.0 109.2 jit_solution(6229760573223545511)
XLA Ops:
  1.9 101.1 %shard_map.101 = (f32[192,2048]{1,0:T(8,128)S(1)}, f32[192,2048]{1,0:T(8,128)S(1)}, f32[192,2048]{1,0:T(8,128)S(1)}, bf16[1536,4096]{1,0:T(8,128)(2,1)S(1)}, bf16[1536,128]{1,0:T(8,128)(2,1)S(1)}) custom-call(f32[1]{0:T(128)S(6)} %copy.11.limit_ref, s32[1]{0:T(128)S(6)} %copy.12.step_ref, f32[192,2048]{1,0:T(8,128)} %master_hbm.1, f32[192,2048]{1,0:T(8,128)} %gradient_hbm.1, ...), custom_call_target="tpu_custom_call" | custom-call | tf_op jit(solution)/shard_map/pallas_call | solution.py:489
  103.0 6.2 %shard_map.102 = (f32[192,2048]{1,0:T(8,128)}, f32[192,2048]{1,0:T(8,128)}, f32[192,2048]{1,0:T(8,128)}, bf16[1536,4096]{1,0:T(8,128)(2,1)}, bf16[1536,128]{1,0:T(8,128)(2,1)}) custom-call(f32[192,2048]{1,0:T(8,128)S(1)} %get-tuple-element.10.refs_0_, f32[192,2048]{1,0:T(8,128)S(1)} %get-tuple-element.11.refs_1_, f32[192,2048]{1,0:T(8,128)S(1)} %get-tuple-element.12.refs_2_, ...), custom_call_target="tpu_custom_call" | custom-call | tf_op jit(solution)/shard_map/pallas_call | solution.py:513

commit v5 on v4

--- a/solution.py
+++ b/solution.py
@@ -20,27 +20,23 @@
 MESH = pl.DeviceIdType.MESH
 Z, Y, X = 0, 1, 2
 PIECES = (
-    ((Z, X, Y), 0, 4),
+    ((Z, X, Y), 0, 5),
+    ((Z, Y, X), 1, 6),
+    ((X, Y, Z), 0, 5),
     ((Y, X, Z), 1, 2),
-    ((Z, Y, X), 0, 4),
-    ((Z, Y, X), 1, 4),
-    ((X, Y, Z), 0, 5),
-    ((Z, X, Y), 1, 6),
-    ((Z, X, Y), 0, 3),
-    ((Z, Y, X), 1, 4),
+    ((Z, Y, X), 0, 6),
+    ((Z, X, Y), 1, 8),
 )
 SCALE_ORDER = (Y, Z, X)
 ROWS = 16
 ITEMS = {
     (4, 2, 2): (
-        (0, 3), (1, 4), (0, 6), (4, 3), (0, 0), (2, 1), (4, 5), (4, 0), (1, 1), (3, 4),
-        (4, 6), (2, 8), (0, 2), (4, 8), (1, 6), (4, 7), (2, 3), (0, 7), (6, 3), (6, 8),
-        (6, 0), (5, 0), (6, 5), (2, 6), (0, 8), (2, 0), (2, 2), (4, 1), (3, 8), (3, 1),
-        (0, 4), (0, 5), (4, 2), (1, 7), (7, 4), (1, 0), (4, 4), (1, 2), (5, 5), (5, 6),
-        (2, 4), (6, 6), (7, 1), (5, 3), (2, 7), (6, 7), (5, 4), (1, 5), (5, 8), (7, 3),
-        (6, 2), (1, 8), (6, 4), (3, 6), (1, 3), (5, 1), (0, 1), (2, 5), (3, 3), (7, 0),
-        (3, 0), (7, 8), (3, 7), (5, 7), (7, 5), (3, 2), (5, 2), (7, 6), (6, 1), (7, 7),
-        (3, 5), (7, 2),
+        (0, 1), (0, 4), (1, 3), (2, 3), (2, 2), (4, 1), (4, 0), (0, 5), (6, 1), (1, 2),
+        (5, 1), (4, 6), (2, 6), (0, 0), (4, 5), (0, 6), (6, 3), (4, 4), (1, 5), (2, 4),
+        (5, 2), (3, 3), (3, 6), (4, 2), (7, 1), (2, 1), (5, 0), (6, 2), (6, 0), (2, 0),
+        (3, 2), (1, 0), (6, 5), (6, 6), (0, 3), (5, 5), (5, 6), (2, 5), (1, 6), (1, 4),
+        (5, 3), (3, 5), (6, 4), (0, 2), (7, 3), (7, 2), (3, 0), (1, 1), (3, 1), (3, 4),
+        (5, 4), (7, 0), (7, 6), (4, 3), (7, 5), (7, 4),
     ),
 }
 WORD = 4
@@ -294,10 +290,8 @@
                 start, size = spans[k]
                 parts = [(0, size, 0, height)]
                 if start == 0:
-                    parts = [(i, 1, 0, height) for i in range(size)]
-                    cut = strips // 2 * ROWS
-                    if cut:
-                        parts[:1] = [(0, 1, 0, cut), (0, 1, cut, height - cut)]
+                    cuts = [0, 1, 3, size] if size > 3 else [0, 1, size]
+                    parts = [(a, b - a, 0, height) for a, b in zip(cuts, cuts[1:])]
                 for offset, part, top_row, rows in parts:
                     begin = start + offset
 

time: 109 us -> 108 us (level)
    pallas_call x1, Pallas kernels: 101 us -> 99.8 us  [per_device(): pl.pallas_call(functools.partial(kernel, grid), out_shape=(state, state,...]
where the time goes in v5:
time: 108 us
  Pallas kernels  106 us (98%)
  between operations  1.93 us (2%)
    pallas_call x1, Pallas kernels, per_device(): pl.pallas_call(functools.partial(kernel, grid), out_shape=(state, state,...  99.8 us
    pallas_call x1, Pallas kernels, per_device(): pl.pallas_call(flush, out_shape=tuple((jax.ShapeDtypeStruct(r.shape, r.dt...  6.24 us

profile of v5, /device:TPU:1, one launch (start us, length us, event | category | flops | bytes accessed | tf_op | source)
XLA Modules:
  0.0 108.0 jit_solution(14782693665312195936)
XLA Ops:
  1.9 99.8 %shard_map.101 = (f32[192,2048]{1,0:T(8,128)S(1)}, f32[192,2048]{1,0:T(8,128)S(1)}, f32[192,2048]{1,0:T(8,128)S(1)}, bf16[1536,4096]{1,0:T(8,128)(2,1)S(1)}, bf16[1536,128]{1,0:T(8,128)(2,1)S(1)}) custom-call(f32[1]{0:T(128)S(6)} %copy.11.limit_ref, s32[1]{0:T(128)S(6)} %copy.12.step_ref, f32[192,2048]{1,0:T(8,128)} %master_hbm.1, f32[192,2048]{1,0:T(8,128)} %gradient_hbm.1, ...), custom_call_target="tpu_custom_call" | custom-call | tf_op jit(solution)/shard_map/pallas_call | solution.py:483
  101.8 6.2 %shard_map.102 = (f32[192,2048]{1,0:T(8,128)}, f32[192,2048]{1,0:T(8,128)}, f32[192,2048]{1,0:T(8,128)}, bf16[1536,4096]{1,0:T(8,128)(2,1)}, bf16[1536,128]{1,0:T(8,128)(2,1)}) custom-call(f32[192,2048]{1,0:T(8,128)S(1)} %get-tuple-element.10.refs_0_, f32[192,2048]{1,0:T(8,128)S(1)} %get-tuple-element.11.refs_1_, f32[192,2048]{1,0:T(8,128)S(1)} %get-tuple-element.12.refs_2_, ...), custom_call_target="tpu_custom_call" | custom-call | tf_op jit(solution)/shard_map/pallas_call | solution.py:507

commit v6 on v5

--- a/solution.py
+++ b/solution.py
@@ -31,12 +31,12 @@
 ROWS = 16
 ITEMS = {
     (4, 2, 2): (
-        (0, 1), (0, 4), (1, 3), (2, 3), (2, 2), (4, 1), (4, 0), (0, 5), (6, 1), (1, 2),
-        (5, 1), (4, 6), (2, 6), (0, 0), (4, 5), (0, 6), (6, 3), (4, 4), (1, 5), (2, 4),
-        (5, 2), (3, 3), (3, 6), (4, 2), (7, 1), (2, 1), (5, 0), (6, 2), (6, 0), (2, 0),
-        (3, 2), (1, 0), (6, 5), (6, 6), (0, 3), (5, 5), (5, 6), (2, 5), (1, 6), (1, 4),
-        (5, 3), (3, 5), (6, 4), (0, 2), (7, 3), (7, 2), (3, 0), (1, 1), (3, 1), (3, 4),
-        (5, 4), (7, 0), (7, 6), (4, 3), (7, 5), (7, 4),
+        (0, 0), (0, 1), (4, 1), (0, 4), (4, 0), (0, 5), (4, 5), (2, 2), (2, 6), (0, 6),
+        (2, 3), (4, 4), (3, 3), (1, 2), (3, 2), (1, 0), (6, 6), (2, 0), (5, 0), (1, 5),
+        (5, 5), (7, 3), (1, 3), (2, 1), (0, 2), (1, 1), (5, 1), (2, 4), (6, 0), (1, 4),
+        (5, 2), (6, 3), (4, 3), (3, 0), (7, 6), (6, 4), (3, 6), (4, 6), (5, 3), (3, 1),
+        (4, 2), (6, 1), (2, 5), (7, 0), (7, 2), (6, 2), (3, 4), (5, 6), (6, 5), (1, 6),
+        (3, 5), (7, 4), (5, 4), (0, 3), (7, 5), (7, 1),
     ),
 }
 WORD = 4
@@ -218,10 +218,10 @@
         at[column] += spans[-1][1]
     assert at == [tiles, tiles]
 
-    def code_part(source, column, start, size, top_row=0, rows=height):
-        row = (chip_at(source) % sources) * height + top_row
+    def code_part(source, column, start, size):
+        row = (chip_at(source) % sources) * height
         lane = column * width + start * LANES
-        return codes.at[pl.ds(pl.multiple_of(row, ROWS), rows), pl.ds(lane, size * LANES)]
+        return codes.at[pl.ds(pl.multiple_of(row, ROWS), height), pl.ds(lane, size * LANES)]
 
     def code_slice(source, k):
         return code_part(source, PIECES[k][1], *spans[k])
@@ -242,10 +242,10 @@
 
     my_index = chip % sources
 
-    def own_copy(column, k, start, size, top_row, rows, to):
+    def own_copy(column, k, start, size, to):
         return pltpu.make_async_remote_copy(
-            src_ref=mine.at[pl.ds(top_row, rows), pl.ds(start * LANES, size * LANES)],
-            dst_ref=code_part(here, column, start, size, top_row, rows),
+            src_ref=mine.at[:, pl.ds(start * LANES, size * LANES)],
+            dst_ref=code_part(here, column, start, size),
             send_sem=send_sem, recv_sem=recv_sem.at[my_index, k],
             device_id=(keeper, to), device_id_type=MESH,
         )
@@ -257,9 +257,8 @@
     per_tile = LANES // BLOCK
     assert tiles <= BLOCK
 
-    def tile(j, top_row=0, rows=height):
-        band = pl.ds(top_row, rows)
-        where = (band, pl.ds(pl.multiple_of(j * LANES, LANES), LANES))
+    def tile(j):
+        where = (slice(None), pl.ds(pl.multiple_of(j * LANES, LANES), LANES))
         weight = master[where]
         slope = gradient[where]
         moment = beta_first * first[where] + clip_first * slope
@@ -278,44 +277,53 @@
         scale = jnp.maximum(largest, scale_floor).astype(jnp.bfloat16)
         scale = jnp.dot(scale, spread, preferred_element_type=jnp.float32)
         mine[where] = (weight / scale).astype(jnp.bfloat16)
-        wide_scales[band, :] = jnp.where(lane % BLOCK == j, scale, wide_scales[band, :])
+        wide_scales[...] = jnp.where(lane % BLOCK == j, scale, wide_scales[...])
 
     wide_scales[...] = jnp.zeros_like(wide_scales)
-    sent = jnp.int32(0)
-    for c in range(2):
-        def own_pieces(sent):
-            for k, (order, column, _) in enumerate(PIECES):
-                if column != c:
-                    continue
-                start, size = spans[k]
-                parts = [(0, size, 0, height)]
-                if start == 0:
-                    cuts = [0, 1, 3, size] if size > 3 else [0, 1, size]
-                    parts = [(a, b - a, 0, height) for a, b in zip(cuts, cuts[1:])]
-                for offset, part, top_row, rows in parts:
-                    begin = start + offset
-
-                    def one_tile(j, carry):
-                        tile(j, top_row, rows)
-                        return carry
-
-                    lax.fori_loop(begin, begin + part, one_tile, 0)
-                    amount = part * rows // ROWS
-                    for used, to in children(here, order):
+    parts = ([], [])
+    for k, (_, column, _) in enumerate(PIECES):
+        start, size = spans[k]
+        cuts = [0, size]
+        if start == 0:
+            cuts = [0, 1, 3, size] if size > 3 else [0, 1, size]
+        parts[column].extend((k, start + a, b - a) for a, b in zip(cuts, cuts[1:]))
+    my_ways = {order: children(here, order) for order, _, _ in PIECES}
+
+    def one_tile(j, carry):
+        tile(j)
+        return carry
+
+    def send_part(p, carry):
+        begin, end = jnp.int32(0), jnp.int32(0)
+        for c in range(2):
+            for i, (_, first_tile, count) in enumerate(parts[c]):
+                at = (core == c) & (p == i)
+                begin = jnp.where(at, first_tile, begin)
+                end = jnp.where(at, first_tile + count, end)
+        lax.fori_loop(begin, end, one_tile, 0)
+
+        for c in range(2):
+            for i, (k, first_tile, count) in enumerate(parts[c]):
+                @pl.when((core == c) & (p == i))
+                def _():
+                    for used, to in my_ways[PIECES[k][0]]:
                         @pl.when(used)
                         def _():
-                            own_copy(c, k, begin, part, top_row, rows, to).start()
-
-                        sent = sent + jnp.where(used, amount, 0)
+                            own_copy(c, k, first_tile, count, to).start()
 
                     @pl.when(c != keeper)
                     def _():
-                        own_copy(c, k, begin, part, top_row, rows, chip).start()
-
-                    sent = sent + jnp.where(c != keeper, amount, 0)
-            return sent
-
-        sent = lax.cond(core == c, own_pieces, lambda s: s, sent)
+                        own_copy(c, k, first_tile, count, chip).start()
+
+        return carry
+
+    lax.fori_loop(0, max(len(p) for p in parts), send_part, 0)
+    sent = jnp.int32(0)
+    for k, (order, column, _) in enumerate(PIECES):
+        amount = spans[k][1] * strips
+        for used, _ in my_ways[order]:
+            sent = sent + jnp.where((core == column) & used, amount, 0)
+        sent = sent + jnp.where((core == column) & (column != keeper), amount, 0)
 
     place_row = spread_row % BLOCK
     target = (core * tiles + place_row) * per_tile + spread_row // BLOCK
@@ -399,7 +407,7 @@
         item = (word >> (7 * (t % WORD))) % 128
         return item // 16, item % 16
 
-    def forward(t, sent):
+    def forward(t, carry):
         q, which = item_of(t)
         source = source_of(q)
         index = chip_at(source) % sources
@@ -410,35 +418,35 @@
             def _():
                 wait_bytes(code_slice(source, k), recv_sem.at[index, k])
 
-            for_k = (which == k) & jnp.logical_not(mine_too)
-            ways = children(source, order)
-
-            @pl.when(for_k)
+            @pl.when((which == k) & jnp.logical_not(mine_too))
             def _():
-                for used, to in ways:
+                for used, to in children(source, order):
                     @pl.when(used)
                     def _():
                         code_copy(source, k, to).start()
 
-            for used, _ in ways:
-                sent = sent + jnp.where(for_k & used, spans[k][1] * strips, 0)
-
-        for_scale = (which == pieces) & jnp.logical_not(mine_too)
-        ways = children(source, SCALE_ORDER)
-
-        @pl.when(for_scale)
+        @pl.when((which == pieces) & jnp.logical_not(mine_too))
         def _():
             wait_bytes(scale_slice(source), recv_sem.at[index, pieces])
-            for used, to in ways:
+            for used, to in children(source, SCALE_ORDER):
                 @pl.when(used)
                 def _():
                     scale_copy(source, to).start()
 
-        for used, _ in ways:
-            sent = sent + jnp.where(for_scale & used, strips, 0)
+        return carry
+
+    def passed(q, sent):
+        source = source_of(q)
+        others = chip_at(source) != chip
+        orders = [(order, spans[k][1] * strips) for k, (order, _, _) in enumerate(PIECES)]
+        for order in sorted({order for order, _ in orders} | {SCALE_ORDER}):
+            amount = sum(a for o, a in orders if o == order) + (order == SCALE_ORDER) * strips
+            for used, _ in children(source, order):
+                sent = sent + jnp.where(others & used, amount, 0)
         return sent
 
-    sent = lax.fori_loop(0, sources * (pieces + 1), forward, sent)
+    sent = lax.fori_loop(0, sources, passed, sent)
+    lax.fori_loop(0, sources * (pieces + 1), forward, 0)
 
     @pl.when(core == keeper)
     def _():

time: 108 us -> 108 us (level)
  no operation moved by 1% of the time
where the time goes in v6:
time: 108 us
  Pallas kernels  106 us (98%)
  between operations  1.93 us (2%)
    pallas_call x1, Pallas kernels, per_device(): pl.pallas_call(functools.partial(kernel, grid), out_shape=(state, state,...  99.6 us
    pallas_call x1, Pallas kernels, per_device(): pl.pallas_call(flush, out_shape=tuple((jax.ShapeDtypeStruct(r.shape, r.dt...  6.24 us

profile of v6, /device:TPU:1, one launch (start us, length us, event | category | flops | bytes accessed | tf_op | source)
XLA Modules:
  0.0 107.8 jit_solution(4570197971254791647)
XLA Ops:
  1.9 99.6 %shard_map.101 = (f32[192,2048]{1,0:T(8,128)S(1)}, f32[192,2048]{1,0:T(8,128)S(1)}, f32[192,2048]{1,0:T(8,128)S(1)}, bf16[1536,4096]{1,0:T(8,128)(2,1)S(1)}, bf16[1536,128]{1,0:T(8,128)(2,1)S(1)}) custom-call(f32[1]{0:T(128)S(6)} %copy.11.limit_ref, s32[1]{0:T(128)S(6)} %copy.12.step_ref, f32[192,2048]{1,0:T(8,128)} %master_hbm.1, f32[192,2048]{1,0:T(8,128)} %gradient_hbm.1, ...), custom_call_target="tpu_custom_call" | custom-call | tf_op jit(solution)/shard_map/pallas_call | solution.py:491
  101.6 6.2 %shard_map.102 = (f32[192,2048]{1,0:T(8,128)}, f32[192,2048]{1,0:T(8,128)}, f32[192,2048]{1,0:T(8,128)}, bf16[1536,4096]{1,0:T(8,128)(2,1)}, bf16[1536,128]{1,0:T(8,128)(2,1)}) custom-call(f32[192,2048]{1,0:T(8,128)S(1)} %get-tuple-element.10.refs_0_, f32[192,2048]{1,0:T(8,128)S(1)} %get-tuple-element.11.refs_1_, f32[192,2048]{1,0:T(8,128)S(1)} %get-tuple-element.12.refs_2_, ...), custom_call_target="tpu_custom_call" | custom-call | tf_op jit(solution)/shard_map/pallas_call | solution.py:515

commit v7 on v6

--- a/solution.py
+++ b/solution.py
@@ -144,14 +144,16 @@
         0, height // 8, square, tuple(jnp.zeros((8, LANES), jnp.float32) for _ in range(4))
     )
     total = (totals[0] + totals[1]) + (totals[2] + totals[3])
-    total = jnp.sum(total, axis=0, keepdims=True)
+    total = jnp.sum(jnp.sum(total, axis=0, keepdims=True), axis=1, keepdims=True)
+    total = jnp.broadcast_to(total, (1, LANES))
 
     one = jnp.ones((1, 1), jnp.float32)
     first_gain = one / (one - power(beta_first, step_ref[0]))
     second_gain = one / (one - power(beta_second, step_ref[0]))
     step_gain = jnp.broadcast_to(learn_rate * first_gain, (1, LANES))
     second_gain = jnp.broadcast_to(second_gain, (1, LANES))
-    norm_limit = jnp.full((1, 1), limit_ref[0], jnp.float32)
+    norm_limit = jnp.full((1, LANES), limit_ref[0], jnp.float32)
+    wide_scales[...] = jnp.zeros_like(wide_scales)
 
     pl.semaphore_wait(barrier, greeted)
 
@@ -175,7 +177,6 @@
         lax.fori_loop(0, count, send, 0)
         others = buffer.at[pl.ds(0, count - 1)]
         wait_bytes(others, recv)
-        wait_bytes(others, sum_send)
         return jnp.sum(buffer[pl.ds(0, count)], axis=0)
 
     total = exchange(total, group_sums, my_place, group, member, group_recv)
@@ -184,9 +185,7 @@
             total, line_sums, here[Z], depth,
             lambda other: (core, chip_at((other, here[Y], here[X]))), line_recv,
         )
-    squares = jnp.sum(total, axis=1, keepdims=True)
-    clip_factor = norm_limit / jnp.maximum(jnp.sqrt(squares), norm_limit)
-    clip_factor = jnp.broadcast_to(clip_factor, (1, LANES))
+    clip_factor = norm_limit / jnp.maximum(jnp.sqrt(total), norm_limit)
     clip_first = (1.0 - beta_first) * clip_factor
     clip_second = (1.0 - beta_second) * clip_factor * clip_factor
     for load in loads[1:]:
@@ -279,7 +278,6 @@
         mine[where] = (weight / scale).astype(jnp.bfloat16)
         wide_scales[...] = jnp.where(lane % BLOCK == j, scale, wide_scales[...])
 
-    wide_scales[...] = jnp.zeros_like(wide_scales)
     parts = ([], [])
     for k, (_, column, _) in enumerate(PIECES):
         start, size = spans[k]
@@ -447,6 +445,10 @@
 
     sent = lax.fori_loop(0, sources, passed, sent)
     lax.fori_loop(0, sources * (pieces + 1), forward, 0)
+
+    wait_bytes(group_sums.at[pl.ds(0, group - 1)], sum_send)
+    if not one_stage:
+        wait_bytes(line_sums.at[pl.ds(0, depth - 1)], sum_send)
 
     @pl.when(core == keeper)
     def _():

time: 108 us -> 108 us (level)
  no operation moved by 1% of the time
where the time goes in v7:
time: 108 us
  Pallas kernels  106 us (98%)
  between operations  1.93 us (2%)
    pallas_call x1, Pallas kernels, per_device(): pl.pallas_call(functools.partial(kernel, grid), out_shape=(state, state,...  99.6 us
    pallas_call x1, Pallas kernels, per_device(): pl.pallas_call(flush, out_shape=tuple((jax.ShapeDtypeStruct(r.shape, r.dt...  6.24 us

profile of v7, /device:TPU:1, one launch (start us, length us, event | category | flops | bytes accessed | tf_op | source)
XLA Modules:
  0.0 107.7 jit_solution(3152402366669988883)
XLA Ops:
  1.9 99.6 %shard_map.101 = (f32[192,2048]{1,0:T(8,128)S(1)}, f32[192,2048]{1,0:T(8,128)S(1)}, f32[192,2048]{1,0:T(8,128)S(1)}, bf16[1536,4096]{1,0:T(8,128)(2,1)S(1)}, bf16[1536,128]{1,0:T(8,128)(2,1)S(1)}) custom-call(f32[1]{0:T(128)S(6)} %copy.11.limit_ref, s32[1]{0:T(128)S(6)} %copy.12.step_ref, f32[192,2048]{1,0:T(8,128)} %master_hbm.1, f32[192,2048]{1,0:T(8,128)} %gradient_hbm.1, ...), custom_call_target="tpu_custom_call" | custom-call | tf_op jit(solution)/shard_map/pallas_call | solution.py:493
  101.5 6.2 %shard_map.102 = (f32[192,2048]{1,0:T(8,128)}, f32[192,2048]{1,0:T(8,128)}, f32[192,2048]{1,0:T(8,128)}, bf16[1536,4096]{1,0:T(8,128)(2,1)}, bf16[1536,128]{1,0:T(8,128)(2,1)}) custom-call(f32[192,2048]{1,0:T(8,128)S(1)} %get-tuple-element.10.refs_0_, f32[192,2048]{1,0:T(8,128)S(1)} %get-tuple-element.11.refs_1_, f32[192,2048]{1,0:T(8,128)S(1)} %get-tuple-element.12.refs_2_, ...), custom_call_target="tpu_custom_call" | custom-call | tf_op jit(solution)/shard_map/pallas_call | solution.py:517

commit v8 on v7

--- a/solution.py
+++ b/solution.py
@@ -252,7 +252,6 @@
     lane = lax.broadcasted_iota(jnp.int32, (1, LANES), 1)
     spread_row = lax.broadcasted_iota(jnp.int32, (LANES, LANES), 0)
     spread_column = lax.broadcasted_iota(jnp.int32, (LANES, LANES), 1)
-    spread = (spread_row == spread_column // BLOCK * BLOCK).astype(jnp.float32).astype(jnp.bfloat16)
     per_tile = LANES // BLOCK
     assert tiles <= BLOCK
 
@@ -271,10 +270,12 @@
         largest = jnp.abs(weight)
         shift = BLOCK // 2
         while shift:
-            largest = jnp.maximum(largest, pltpu.roll(largest, LANES - shift, axis=1))
+            ahead = pltpu.roll(largest, LANES - shift, axis=1)
+            behind = pltpu.roll(largest, shift, axis=1)
+            largest = jnp.maximum(largest, jnp.where((lane & shift) == 0, ahead, behind))
             shift //= 2
         scale = jnp.maximum(largest, scale_floor).astype(jnp.bfloat16)
-        scale = jnp.dot(scale, spread, preferred_element_type=jnp.float32)
+        scale = scale.astype(jnp.float32)
         mine[where] = (weight / scale).astype(jnp.bfloat16)
         wide_scales[...] = jnp.where(lane % BLOCK == j, scale, wide_scales[...])
 

time: 108 us -> 108 us (level)
  no operation moved by 1% of the time
where the time goes in v8:
time: 108 us
  Pallas kernels  106 us (98%)
  between operations  1.93 us (2%)
    pallas_call x1, Pallas kernels, per_device(): pl.pallas_call(functools.partial(kernel, grid), out_shape=(state, state,...  99.5 us
    pallas_call x1, Pallas kernels, per_device(): pl.pallas_call(flush, out_shape=tuple((jax.ShapeDtypeStruct(r.shape, r.dt...  6.24 us

profile of v8, /device:TPU:1, one launch (start us, length us, event | category | flops | bytes accessed | tf_op | source)
XLA Modules:
  0.0 107.6 jit_solution(3250922131674431537)
XLA Ops:
  1.9 99.5 %shard_map.101 = (f32[192,2048]{1,0:T(8,128)S(1)}, f32[192,2048]{1,0:T(8,128)S(1)}, f32[192,2048]{1,0:T(8,128)S(1)}, bf16[1536,4096]{1,0:T(8,128)(2,1)S(1)}, bf16[1536,128]{1,0:T(8,128)(2,1)S(1)}) custom-call(f32[1]{0:T(128)S(6)} %copy.11.limit_ref, s32[1]{0:T(128)S(6)} %copy.12.step_ref, f32[192,2048]{1,0:T(8,128)} %master_hbm.1, f32[192,2048]{1,0:T(8,128)} %gradient_hbm.1, ...), custom_call_target="tpu_custom_call" | custom-call | tf_op jit(solution)/shard_map/pallas_call | solution.py:494
  101.4 6.2 %shard_map.102 = (f32[192,2048]{1,0:T(8,128)}, f32[192,2048]{1,0:T(8,128)}, f32[192,2048]{1,0:T(8,128)}, bf16[1536,4096]{1,0:T(8,128)(2,1)}, bf16[1536,128]{1,0:T(8,128)(2,1)}) custom-call(f32[192,2048]{1,0:T(8,128)S(1)} %get-tuple-element.10.refs_0_, f32[192,2048]{1,0:T(8,128)S(1)} %get-tuple-element.11.refs_1_, f32[192,2048]{1,0:T(8,128)S(1)} %get-tuple-element.12.refs_2_, ...), custom_call_target="tpu_custom_call" | custom-call | tf_op jit(solution)/shard_map/pallas_call | solution.py:518
